TPU v7x, 32 devices: a whole 2x2x4 slice. The times are simulated.
32 devices in a mesh: aa: 4 (over y, core), ba: 2 (over x), col: 4 (over z).
Axes of the slice: x: 2, y: 2, z: 4, core: 2. Of those that a mesh axis runs over, the one named last changes fastest.
Arguments:
- right_side: float32 [4, 384, 384, 384], P(None, 'aa', 'ba', 'col'), may hold values from -6 to 6
- shift: float32 [4], replicated, may hold values from 0.5 to 4
Outputs:
- solution: float32 [4, 384, 384, 384], P(None, 'aa', 'ba', 'col')
All inputs are finite; a program needn't handle non-finite values.
Results may differ from a plain program's by a relative error of at most 0.0003.
Values sent between devices are 32-bit elements.
A program may use at most 256 MiB of HBM per device.

v0:
```python
import math

import jax
import jax.numpy as jnp
from jax import lax
from jax.sharding import PartitionSpec as P

NX = 384
NY = 384
NZ = 384


def dct_matrix(length):
    freq_ids = jnp.arange(length, dtype=jnp.float32)[:, None]
    cell_ids = jnp.arange(length, dtype=jnp.float32)[None, :]
    weights = jnp.where(
        freq_ids == 0.0, jnp.float32(math.sqrt(1.0 / length)), jnp.float32(math.sqrt(2.0 / length))
    )
    return weights * jnp.cos(
        jnp.float32(math.pi) * freq_ids * (2.0 * cell_ids + 1.0) / (2.0 * length)
    )


def eigen_at(global_ids, length):
    return 2.0 - 2.0 * jnp.cos(jnp.float32(math.pi) * global_ids.astype(jnp.float32) / length)


def transform(field, matrix, which_dim):
    patterns = ["bnyz,kn->bkyz", "bxnz,kn->bxkz", "bxyn,kn->bxyk"]
    return jnp.einsum(patterns[which_dim - 1], field, matrix, precision=lax.Precision.HIGHEST)


def divide_modes(widened, shift_part, first_ids, third_ids):
    denominator = (
        eigen_at(first_ids, NX)[None, :, None, None]
        + eigen_at(jnp.arange(NY, dtype=jnp.int32), NY)[None, None, :, None]
        + eigen_at(third_ids, NZ)[None, None, None, :]
        + shift_part[:, None, None, None]
    )
    return widened / denominator


def first_batched(field, matrix):
    widened = lax.all_to_all(field, "aa", split_axis=3, concat_axis=1, tiled=True)
    widened = transform(widened, matrix, 1)
    return lax.all_to_all(widened, "aa", split_axis=1, concat_axis=3, tiled=True)


def per_device(right_side, shift):
    along_first = dct_matrix(NX)
    along_second = dct_matrix(NY)
    along_third = dct_matrix(NZ)
    local_first = right_side.shape[1]
    first_ids = lax.axis_index("aa") * local_first + jnp.arange(local_first, dtype=jnp.int32)
    batch_rows = right_side.shape[0] // lax.axis_size("col")
    shift_part = lax.dynamic_slice_in_dim(shift, lax.axis_index("col") * batch_rows, batch_rows)
    third_part = NZ // lax.axis_size("ba")
    third_ids = lax.axis_index("ba") * third_part + jnp.arange(third_part, dtype=jnp.int32)
    field = lax.all_to_all(right_side, "col", split_axis=0, concat_axis=3, tiled=True)
    field = transform(field, along_third, 3)
    field = first_batched(field, along_first)
    widened = lax.all_to_all(field, "ba", split_axis=3, concat_axis=2, tiled=True)
    widened = transform(widened, along_second, 2)
    widened = divide_modes(widened, shift_part, first_ids, third_ids)
    widened = transform(widened, along_second.T, 2)
    field = lax.all_to_all(widened, "ba", split_axis=2, concat_axis=3, tiled=True)
    field = first_batched(field, along_first.T)
    field = transform(field, along_third.T, 3)
    solution = lax.all_to_all(field, "col", split_axis=3, concat_axis=0, tiled=True)
    return solution


def solution(mesh):
    in_specs = (P(None, "aa", "ba", "col"), P())
    out_specs = P(None, "aa", "ba", "col")
    return jax.shard_map(
        per_device, mesh=mesh, in_specs=in_specs, out_specs=out_specs, check_vma=False
    )
```

profile of v0, /device:TPU:7, one launch (start us, length us, event | category | flops | bytes accessed | tf_op | source)
XLA Modules:
  0.0 5510.6 jit_solution(15054527832602330240)
XLA Ops:
  0.0 10.5 all-to-all-start
  10.6 811.6 %all-to-all-done = f32[4,96,192,96]{3,2,1,0:T(8,128)} async-done(((f32[4,96,192,96]{3,2,1,0:T(8,128)}), f32[4,96,192,96]{3,2,1,0:T(8,128)}, u32[]{:S(2)}, u32[]{:S(2)}) %all-to-all-start) | async-done | bytes 28311584 | tf_op jit(solution)/shard_map/all_to_all | solution.py:59
  822.1 42.6 copy.15
  864.8 38.8 reshape.127
  903.5 74.3 %convolution_bitcast_fusion.1 = f32[1,96,192,384]{3,2,1,0:T(8,128)} fusion(f32[96,192,384]{2,1,0:T(8,128)} %reshape.127, f32[384]{0:T(512)S(1)} %get-tuple-element.5, f32[384]{0:T(512)S(1)} %get-tuple-element.6, f32[384]{0:T(512)S(1)} %fusion.30), kind=kOutput, calls=%fused_computation.6 | convolution fusion | flops 32615350272 | bytes 56627712 | tf_op jit(solution)/shard_map/bxyn,kn->bxyk/dot_general | solution.py:30
  977.9 37.3 copy.16
  1015.2 12.2 all-to-all-start.1
  1027.5 2.0 cosine_multiply_fusion.14
  1029.5 403.8 %all-to-all-done.1 = f32[1,96,192,384]{2,1,0,3:T(8,128)} async-done(((f32[1,96,192,384]{2,1,0,3:T(8,128)}), f32[1,96,192,384]{2,1,0,3:T(8,128)}, u32[]{:S(2)}, u32[]{:S(2)}) %all-to-all-start.1) | async-done | bytes 28311584 | tf_op jit(solution)/shard_map/all_to_all | solution.py:44
  1433.3 49.5 copy.17
  1482.8 38.8 reshape.134
  1521.6 57.3 %fusion.5 = f32[384,18432]{0,1} fusion(f32[384,18432]{0,1:T(8,128)} %reshape.134, f32[384,384]{1,0:T(8,128)S(1)} %cosine_multiply_fusion.14), kind=kOutput, calls=%fused_computation.13 | convolution fusion | flops 32614907904 | bytes 57212928
  1579.0 33.0 copy.18
  1612.0 427.9 %all_to_all.129 = f32[1,384,192,96]{3,2,0,1:T(8,128)} all-to-all(f32[1,384,192,96]{3,2,0,1:T(8,128)} %copy.18), channel_id=1, replica_groups=mesh['aa'=4,'ba'=2,'col'=4] {'aa'}, dimensions={1} | all-to-all | bytes 56623104 | tf_op jit(solution)/shard_map/all_to_all | solution.py:46
  2039.9 42.6 copy.44
  2082.5 40.9 copy.32
  2123.4 14.9 all-to-all-start.3
  2138.3 0.7 dynamic_slice.3
  2139.1 0.1 broadcast_add_fusion
  2139.2 2.0 cosine_multiply_fusion.13
  2141.3 2.0 cosine_multiply_fusion.12
  2143.3 400.2 %all-to-all-done.3 = f32[1,96,192,384]{2,1,0,3:T(8,128)} async-done(((f32[1,96,192,384]{2,1,0,3:T(8,128)}), f32[1,96,192,384]{2,1,0,3:T(8,128)}, u32[]{:S(2)}, u32[]{:S(2)}) %all-to-all-start.3) | async-done | bytes 28311584 | tf_op jit(solution)/shard_map/all_to_all | solution.py:62
  2543.6 62.3 %copy.41 = f32[1,96,192,2,192]{2,3,4,1,0:T(2,128)} copy(f32[1,96,192,2,192]{2,1,4,3,0:T(8,128)} %bitcast.12) | data formatting | bytes 56623104 | tf_op jit(solution)/shard_map/all_to_all | solution.py:62
  2605.8 42.5 reshape.129
  2648.3 57.3 %fusion.4 = f32[384,18432]{0,1} fusion(f32[384,18432]{0,1:T(8,128)} %bitcast.107, f32[384,384]{1,0:T(8,128)S(1)} %cosine_multiply_fusion.13), kind=kOutput, calls=%fused_computation.12 | convolution fusion | flops 32614907904 | bytes 57212928
  2705.7 22.3 add_divide_fusion
  2728.0 57.7 %fusion.3 = f32[384,18432]{0,1} fusion(f32[384,18432]{0,1:T(8,128)} %bitcast.108, f32[384,384]{1,0:T(8,128)S(1)} %cosine_multiply_fusion.12), kind=kOutput, calls=%fused_computation.11 | convolution fusion | flops 32614907904 | bytes 57212928
  2785.7 37.3 copy.23
  2823.0 441.5 %all_to_all.130 = f32[1,96,384,192]{3,1,0,2:T(8,128)} all-to-all(f32[1,96,384,192]{3,1,0,2:T(8,128)} %copy.23), channel_id=1, replica_groups=mesh['aa'=4,'ba'=2,'col'=4] {'ba'}, dimensions={2} | all-to-all | bytes 56623104 | tf_op jit(solution)/shard_map/all_to_all | solution.py:66
  3264.5 61.9 %copy.43 = f32[1,96,2,192,192]{4,2,3,1,0:T(2,128)} copy(f32[1,96,2,192,192]{4,1,3,2,0:T(8,128)} %bitcast.100) | data formatting | bytes 56623104 | tf_op jit(solution)/shard_map/all_to_all | solution.py:66
  3326.4 52.5 copy.35
  3378.9 13.4 all-to-all-start.5
  3392.3 2.0 cosine_multiply_fusion.11
  3394.3 403.8 %all-to-all-done.5 = f32[1,96,192,384]{2,1,0,3:T(8,128)} async-done(((f32[1,96,192,384]{2,1,0,3:T(8,128)}), f32[1,96,192,384]{2,1,0,3:T(8,128)}, u32[]{:S(2)}, u32[]{:S(2)}) %all-to-all-start.5) | async-done | bytes 28311584 | tf_op jit(solution)/shard_map/all_to_all | solution.py:44
  3798.1 38.5 copy.36
  3836.6 49.5 copy.27
  3886.1 38.8 reshape.140
  3924.9 57.6 %fusion.2 = f32[384,18432]{0,1} fusion(f32[384,18432]{0,1:T(8,128)} %reshape.140, f32[384,384]{1,0:T(8,128)S(1)} %cosine_multiply_fusion.11), kind=kOutput, calls=%fused_computation.10 | convolution fusion | flops 32614907904 | bytes 57212928
  3982.5 33.0 copy.28
  4015.5 12.5 all-to-all-start.6
  4028.0 2.0 fusion.51
  4030.1 403.8 %all-to-all-done.6 = f32[1,384,192,96]{3,2,0,1:T(8,128)} async-done(((f32[1,384,192,96]{3,2,0,1:T(8,128)}), f32[1,384,192,96]{3,2,0,1:T(8,128)}, u32[]{:S(2)}, u32[]{:S(2)}) %all-to-all-start.6) | async-done | bytes 28311584 | tf_op jit(solution)/shard_map/all_to_all | solution.py:46
  4433.9 42.6 copy.42
  4476.5 38.8 reshape.132
  4515.3 58.3 %convolution_bitcast_fusion = f32[1,96,192,384]{3,2,1,0:T(8,128)} fusion(f32[96,192,384]{2,1,0:T(8,128)} %reshape.132, f32[384,384,1]{1,0,2:T(8,128)S(1)} %fusion.51), kind=kOutput, calls=%fused_computation.5 | convolution fusion | flops 32614907904 | bytes 57212928 | tf_op jit(solution)/shard_map/bxyn,kn->bxyk/dot_general | solution.py:30
  4573.6 37.3 copy.30
  4610.9 859.5 %all_to_all.131 = f32[1,96,192,384]{2,1,0,3:T(8,128)} all-to-all(f32[1,96,192,384]{2,1,0,3:T(8,128)} %copy.30), channel_id=1, replica_groups=mesh['aa'=4,'ba'=2,'col'=4] {'col'}, dimensions={3} | all-to-all | bytes 56623104 | tf_op jit(solution)/shard_map/all_to_all | solution.py:69
  5470.3 40.1 copy.31
  (25 shorter events, 0.2 us)
Async XLA Ops:
  0.0 822.1 %all-to-all-start = ((f32[4,96,192,96]{3,2,1,0:T(8,128)}), f32[4,96,192,96]{3,2,1,0:T(8,128)}, u32[]{:S(2)}, u32[]{:S(2)}) async-start(f32[4,96,192,96]{3,2,1,0:T(8,128)} %param.2), calls=%async_computation | async-start | bytes 75497472 | tf_op jit(solution)/shard_map/all_to_all | solution.py:59
  10.5 1016.9 %copy-start = (f32[384]{0:T(512)}, f32[384]{0:T(512)S(1)}, u32[]{:S(2)}) copy-start(f32[384]{0:T(512)S(1)} %fusion.30) | copy-start | bytes 4612
  10.6 1016.9 %copy-start.3 = (f32[384]{0:T(512)}, f32[384]{0:T(512)S(1)}, u32[]{:S(2)}) copy-start(f32[384]{0:T(512)S(1)} %get-tuple-element.5) | copy-start | bytes 4612
  10.6 1016.9 %copy-start.6 = (f32[384]{0:T(512)}, f32[384]{0:T(512)S(1)}, u32[]{:S(2)}) copy-start(f32[384]{0:T(512)S(1)} %get-tuple-element.6) | copy-start | bytes 4612
  1015.2 418.1 %all-to-all-start.1 = ((f32[1,96,192,384]{2,1,0,3:T(8,128)}), f32[1,96,192,384]{2,1,0,3:T(8,128)}, u32[]{:S(2)}, u32[]{:S(2)}) async-start(f32[1,96,192,384]{2,1,0,3:T(8,128)} %copy.16), calls=%async_computation.1 | async-start | bytes 75497472 | tf_op jit(solution)/shard_map/all_to_all | solution.py:44
  2123.4 15.0 copy-start.9
  2123.4 15.9 copy-start.1
  2123.4 15.9 copy-start.4
  2123.4 15.9 copy-start.7
  2123.4 420.2 %all-to-all-start.3 = ((f32[1,96,192,384]{2,1,0,3:T(8,128)}), f32[1,96,192,384]{2,1,0,3:T(8,128)}, u32[]{:S(2)}, u32[]{:S(2)}) async-start(f32[1,96,192,384]{2,1,0,3:T(8,128)} %bitcast.94), calls=%async_computation.3 | async-start | bytes 75497472 | tf_op jit(solution)/shard_map/all_to_all | solution.py:62
  3378.8 13.4 copy-start.2
  3378.8 13.4 copy-start.5
  3378.9 13.4 copy-start.8
  3378.9 419.3 %all-to-all-start.5 = ((f32[1,96,192,384]{2,1,0,3:T(8,128)}), f32[1,96,192,384]{2,1,0,3:T(8,128)}, u32[]{:S(2)}, u32[]{:S(2)}) async-start(f32[1,96,192,384]{2,1,0,3:T(8,128)} %bitcast.95), calls=%async_computation.5 | async-start | bytes 75497472 | tf_op jit(solution)/shard_map/all_to_all | solution.py:44
  4015.5 418.4 %all-to-all-start.6 = ((f32[1,384,192,96]{3,2,0,1:T(8,128)}), f32[1,384,192,96]{3,2,0,1:T(8,128)}, u32[]{:S(2)}, u32[]{:S(2)}) async-start(f32[1,384,192,96]{3,2,0,1:T(8,128)} %copy.28), calls=%async_computation.6 | async-start | bytes 75497472 | tf_op jit(solution)/shard_map/all_to_all | solution.py:46
where the time goes:
time: 5530 us; the launch traced here: 5510 us
  waiting for transfers between devices  2420 us (44%)
  blocking collectives  1730 us (31%)
  local copies, waits for them, and re-layouts  899 us (16%)
  matrix products  363 us (7%)
  starting transfers between devices  63.6 us (1%)
    all_to_all x1, blocking collectives, per_device(): lax.all_to_all(field, 'col', split_axis=3, concat_axis=0, tiled=True)  859 us
    all_to_all x1, waiting for transfers between devices, per_device(): lax.all_to_all(right_side, 'col', split_axis=0, concat_axis=3, tiled=True)  812 us
    all_to_all x2, waiting for transfers between devices, first_batched(): lax.all_to_all(field, 'aa', split_axis=3, concat_axis=1, tiled=True)  808 us
    all_to_all x1, blocking collectives, per_device(): lax.all_to_all(widened, 'ba', split_axis=2, concat_axis=3, tiled=True)  441 us
    all_to_all x1, blocking collectives, first_batched(): lax.all_to_all(widened, 'aa', split_axis=1, concat_axis=3, tiled=True)  428 us
    all_to_all x1, waiting for transfers between devices, first_batched(): lax.all_to_all(widened, 'aa', split_axis=1, concat_axis=3, tiled=True)  404 us
    all_to_all x1, waiting for transfers between devices, per_device(): lax.all_to_all(field, 'ba', split_axis=3, concat_axis=2, tiled=True)  400 us
    unnamed x4, matrix products  230 us
  transfers between devices with their start and end apart: 5, of which 5 were waited for; matrix products, arithmetic and copies ran while one was open for 0% of the time, Pallas kernels for 0%

commit v1 on v0

v1 whole, which is shorter than its diff:
```python
import math

import jax
import jax.numpy as jnp
from jax import lax
from jax.sharding import PartitionSpec as P

CHUNKS = 1


def dct_matrix(length):
    freq_ids = jnp.arange(length, dtype=jnp.float32)[:, None]
    cell_ids = jnp.arange(length, dtype=jnp.float32)[None, :]
    weights = jnp.where(
        freq_ids == 0.0, jnp.float32(math.sqrt(1.0 / length)), jnp.float32(math.sqrt(2.0 / length))
    )
    return weights * jnp.cos(
        jnp.float32(math.pi) * freq_ids * (2.0 * cell_ids + 1.0) / (2.0 * length)
    )


def eigen_at(global_ids, length):
    return 2.0 - 2.0 * jnp.cos(jnp.float32(math.pi) * global_ids.astype(jnp.float32) / length)


def transform(field, matrix, which_dim):
    patterns = ["bnyz,kn->bkyz", "bxnz,kn->bxkz", "bxyn,kn->bxyk"]
    return jnp.einsum(patterns[which_dim - 1], field, matrix, precision=lax.Precision.HIGH)


def exchange(field, axis, split, concat):
    return lax.all_to_all(field, axis, split_axis=split, concat_axis=concat, tiled=True)


def per_device(right_side, shift):
    nx = right_side.shape[1] * lax.axis_size("aa")
    ny = right_side.shape[2] * lax.axis_size("ba")
    nz = right_side.shape[3] * lax.axis_size("col")
    along_first = dct_matrix(nx)
    along_second = dct_matrix(ny)
    along_third = dct_matrix(nz)
    batch_rows = right_side.shape[0] // lax.axis_size("col")
    shift_part = lax.dynamic_slice_in_dim(shift, lax.axis_index("col") * batch_rows, batch_rows)
    first_part = nx // lax.axis_size("ba")
    first_ids = lax.axis_index("ba") * first_part + jnp.arange(first_part, dtype=jnp.int32)
    chunk = nz // CHUNKS
    third_part = chunk // lax.axis_size("aa")

    field = exchange(right_side, "col", 0, 3)
    parts = []
    for c in range(CHUNKS):
        third_ids = (
            c * chunk
            + lax.axis_index("aa") * third_part
            + jnp.arange(third_part, dtype=jnp.int32)
        )
        part = transform(field, along_third[c * chunk : (c + 1) * chunk], 3)
        part = exchange(part, "aa", 3, 1)
        part = transform(part, along_first, 1)
        part = exchange(part, "ba", 1, 2)
        part = transform(part, along_second, 2)
        denominator = (
            eigen_at(first_ids, nx)[None, :, None, None]
            + eigen_at(jnp.arange(ny, dtype=jnp.int32), ny)[None, None, :, None]
            + eigen_at(third_ids, nz)[None, None, None, :]
            + shift_part[:, None, None, None]
        )
        part = part / denominator
        part = transform(part, along_second.T, 2)
        part = exchange(part, "ba", 2, 1)
        part = transform(part, along_first.T, 1)
        parts.append(exchange(part, "aa", 1, 3))
    field = parts[0] if CHUNKS == 1 else jnp.concatenate(parts, axis=3)
    field = transform(field, along_third.T, 3)
    return exchange(field, "col", 3, 0)


def solution(mesh):
    spec = P(None, "aa", "ba", "col")
    return jax.shard_map(
        per_device, mesh=mesh, in_specs=(spec, P()), out_specs=spec, check_vma=False
    )
```

time: 5530 us -> 4350 us (0.79)
  waiting for transfers between devices: 2420 us -> 1220 us
  blocking collectives: 1730 us -> 2140 us
  local copies, waits for them, and re-layouts: 899 us -> 655 us
  matrix products: 363 us -> 269 us
    all_to_all x5 -> x2, waiting for transfers between devices: 2420 us -> 1220 us  [exchange(): lax.all_to_all(field, axis, split_axis=split, concat_axis=concat, tiled=T...]
    all_to_all x3 -> x4, blocking collectives: 1730 us -> 2140 us  [exchange(): lax.all_to_all(field, axis, split_axis=split, concat_axis=concat, tiled=T...]
    all_to_all x11 -> x6, local copies, waits for them, and re-layouts: 523 us -> 279 us  [exchange(): lax.all_to_all(field, axis, split_axis=split, concat_axis=concat, tiled=T...]
  transfers between devices with their start and end apart: 5 -> 2, of which waited for: 5 -> 2; matrix products, arithmetic and copies ran while one was open for 0% -> 0% of each run, Pallas kernels for 0% -> 0%
where the time goes in v1:
time: 4350 us; the launch traced here: 4330 us
  blocking collectives  2140 us (49%)
  waiting for transfers between devices  1220 us (28%)
  local copies, waits for them, and re-layouts  655 us (15%)
  matrix products  269 us (6%)
    all_to_all x4, blocking collectives, exchange(): lax.all_to_all(field, axis, split_axis=split, concat_axis=concat, tiled=T...  2140 us
    all_to_all x2, waiting for transfers between devices, exchange(): lax.all_to_all(field, axis, split_axis=split, concat_axis=concat, tiled=T...  1220 us
    all_to_all x6, local copies, waits for them, and re-layouts, exchange(): lax.all_to_all(field, axis, split_axis=split, concat_axis=concat, tiled=T...  279 us
    unnamed x4, matrix products  182 us
    transpose x3, local copies, waits for them, and re-layouts, transform(): jnp.einsum(patterns[which_dim - 1], field, matrix, precision=lax.Precisio...  99 us
    dot_general x2, matrix products, transform(): jnp.einsum(patterns[which_dim - 1], field, matrix, precision=lax.Precisio...  87.3 us
  transfers between devices with their start and end apart: 2, of which 2 were waited for; matrix products, arithmetic and copies ran while one was open for 0% of the time, Pallas kernels for 0%

profile of v1, /device:TPU:7, one launch (start us, length us, event | category | flops | bytes accessed | tf_op | source)
XLA Modules:
  0.0 4330.3 jit_solution(4623778968149370919)
XLA Ops:
  0.0 10.5 all-to-all-start
  10.5 811.7 %all-to-all-done = f32[4,96,192,96]{3,2,1,0:T(8,128)} async-done(((f32[4,96,192,96]{3,2,1,0:T(8,128)}), f32[4,96,192,96]{3,2,1,0:T(8,128)}, u32[]{:S(2)}, u32[]{:S(2)}) %all-to-all-start) | async-done | bytes 28311584 | tf_op jit(solution)/shard_map/all_to_all | solution.py:32
  822.2 42.6 copy.9
  864.8 38.7 reshape.127
  903.5 43.6 %convolution_bitcast_fusion.1 = f32[1,96,192,384]{3,2,1,0:T(8,128)} fusion(f32[96,192,384]{2,1,0:T(8,128)} %reshape.127, f32[384]{0:T(512)S(1)} %get-tuple-element.5, f32[384]{0:T(512)S(1)} %get-tuple-element.6, f32[384]{0:T(512)S(1)} %fusion.30), kind=kOutput, calls=%fused_computation.3 | convolution fusion | flops 16307896320 | bytes 56627712 | tf_op jit(solution)/shard_map/bxyn,kn->bxyk/dot_general | solution.py:28
  947.1 37.3 copy.10
  984.4 427.5 %all_to_all.93 = f32[1,96,192,384]{2,1,0,3:T(8,128)} all-to-all(f32[1,96,192,384]{2,1,0,3:T(8,128)} %copy.10), channel_id=1, replica_groups=mesh['aa'=4,'ba'=2,'col'=4] {'aa'}, dimensions={3} | all-to-all | bytes 56623104 | tf_op jit(solution)/shard_map/all_to_all | solution.py:32
  1411.9 49.5 %copy.11 = f32[1,96,192,4,96]{1,3,4,2,0:T(4,128)} copy(f32[1,96,192,4,96]{2,1,4,3,0:T(8,128)} %bitcast.65) | data formatting | bytes 56623104 | tf_op jit(solution)/shard_map/all_to_all | solution.py:32
  1461.5 38.7 reshape.134
  1500.2 45.4 %fusion.5 = f32[384,18432]{0,1} fusion(f32[384,18432]{0,1:T(8,128)} %reshape.134, f32[384]{0:T(512)S(1)} %get-tuple-element.5, f32[384]{0:T(512)S(1)} %get-tuple-element.6, f32[384]{0:T(512)S(1)} %fusion.30), kind=kOutput, calls=%fused_computation.10 | convolution fusion | flops 16307896320 | bytes 56627712
  1545.6 33.0 copy.12
  1578.6 0.0 copy-start
  1578.6 15.3 all-to-all-start.2
  1593.9 0.0 copy-done
  1593.9 0.6 dynamic_slice.3
  1594.7 0.1 broadcast_add_fusion
  1594.8 404.4 %all-to-all-done.2 = f32[1,384,192,96]{3,2,0,1:T(8,128)} async-done(((f32[1,384,192,96]{3,2,0,1:T(8,128)}), f32[1,384,192,96]{3,2,0,1:T(8,128)}, u32[]{:S(2)}, u32[]{:S(2)}) %all-to-all-start.2) | async-done | bytes 28311584 | tf_op jit(solution)/shard_map/all_to_all | solution.py:32
  1999.2 52.2 %copy.13 = f32[1,2,192,192,96]{3,1,4,2,0:T(2,128)} copy(f32[1,2,192,192,96]{4,3,2,1,0:T(8,128)} %bitcast.9) | data formatting | bytes 56623104 | tf_op jit(solution)/shard_map/all_to_all | solution.py:32
  2051.4 42.5 reshape.129
  2093.9 45.5 %fusion.4 = f32[384,18432]{0,1} fusion(f32[384,18432]{0,1:T(8,128)} %bitcast.76, f32[384]{0:T(512)S(1)} %get-tuple-element.5, f32[384]{0:T(512)S(1)} %get-tuple-element.6, f32[384]{0:T(512)S(1)} %fusion.30), kind=kOutput, calls=%fused_computation.9 | convolution fusion | flops 16307896320 | bytes 56627712
  2139.4 22.4 add_divide_fusion
  2161.8 45.6 %fusion.3 = f32[384,18432]{0,1} fusion(f32[384,18432]{0,1:T(8,128)} %bitcast.74, f32[384]{0:T(512)S(1)} %get-tuple-element.5, f32[384]{0:T(512)S(1)} %get-tuple-element.6, f32[384]{0:T(512)S(1)} %fusion.30), kind=kOutput, calls=%fused_computation.8 | convolution fusion | flops 16307896320 | bytes 56627712
  2207.4 33.0 copy.14
  2240.4 441.6 %all_to_all.94 = f32[1,192,384,96]{3,1,0,2:T(8,128)} all-to-all(f32[1,192,384,96]{3,1,0,2:T(8,128)} %copy.14), channel_id=1, replica_groups=mesh['aa'=4,'ba'=2,'col'=4] {'ba'}, dimensions={2} | all-to-all | bytes 56623104 | tf_op jit(solution)/shard_map/all_to_all | solution.py:32
  2682.0 52.2 %copy.15 = f32[1,192,2,192,96]{1,2,4,3,0:T(2,128)} copy(f32[1,192,2,192,96]{4,1,3,2,0:T(8,128)} %bitcast.68) | data formatting | bytes 56623104 | tf_op jit(solution)/shard_map/all_to_all | solution.py:32
  2734.2 42.5 reshape.140
  2776.7 45.4 %fusion.2 = f32[384,18432]{0,1} fusion(f32[384,18432]{0,1:T(8,128)} %reshape.140, f32[384]{0:T(512)S(1)} %get-tuple-element.5, f32[384]{0:T(512)S(1)} %get-tuple-element.6, f32[384]{0:T(512)S(1)} %fusion.30), kind=kOutput, calls=%fused_computation.7 | convolution fusion | flops 16307896320 | bytes 56627712
  2822.1 33.0 copy.16
  2855.1 428.4 %all_to_all.95 = f32[1,384,192,96]{3,2,0,1:T(8,128)} all-to-all(f32[1,384,192,96]{3,2,0,1:T(8,128)} %copy.16), channel_id=1, replica_groups=mesh['aa'=4,'ba'=2,'col'=4] {'aa'}, dimensions={1} | all-to-all | bytes 56623104 | tf_op jit(solution)/shard_map/all_to_all | solution.py:32
  3283.5 42.6 copy.21
  3326.1 38.7 reshape.132
  3364.8 43.6 %convolution_bitcast_fusion = f32[1,96,192,384]{3,2,1,0:T(8,128)} fusion(f32[96,192,384]{2,1,0:T(8,128)} %reshape.132, f32[384]{0:T(512)S(1)} %get-tuple-element.5, f32[384]{0:T(512)S(1)} %get-tuple-element.6, f32[384]{0:T(512)S(1)} %fusion.30), kind=kOutput, calls=%fused_computation.2 | convolution fusion | flops 16307896320 | bytes 56627712 | tf_op jit(solution)/shard_map/bxyn,kn->bxyk/dot_general | solution.py:28
  3408.5 37.3 copy.18
  3445.7 844.0 %all_to_all.96 = f32[1,96,192,384]{2,1,0,3:T(8,128)} all-to-all(f32[1,96,192,384]{2,1,0,3:T(8,128)} %copy.18), channel_id=1, replica_groups=mesh['aa'=4,'ba'=2,'col'=4] {'col'}, dimensions={3} | all-to-all | bytes 56623104 | tf_op jit(solution)/shard_map/all_to_all | solution.py:32
  4289.8 40.1 copy.19
  (5 shorter events, 0.2 us)
Async XLA Ops:
  0.0 822.2 %all-to-all-start = ((f32[4,96,192,96]{3,2,1,0:T(8,128)}), f32[4,96,192,96]{3,2,1,0:T(8,128)}, u32[]{:S(2)}, u32[]{:S(2)}) async-start(f32[4,96,192,96]{3,2,1,0:T(8,128)} %param.2), calls=%async_computation | async-start | bytes 75497472 | tf_op jit(solution)/shard_map/all_to_all | solution.py:32
  1578.6 15.3 copy-start
  1578.6 420.6 %all-to-all-start.2 = ((f32[1,384,192,96]{3,2,0,1:T(8,128)}), f32[1,384,192,96]{3,2,0,1:T(8,128)}, u32[]{:S(2)}, u32[]{:S(2)}) async-start(f32[1,384,192,96]{3,2,0,1:T(8,128)} %copy.12), calls=%async_computation.2 | async-start | bytes 75497472 | tf_op jit(solution)/shard_map/all_to_all | solution.py:32
